TPU v7x, 32 devices: a whole 2x2x4 slice. The times are simulated.
32 devices in a mesh: gx: 4 (over y, x), gy: 8 (over z, core).
Axes of the slice: x: 2, y: 2, z: 4, core: 2. Of those that a mesh axis runs over, the one named last changes fastest.
Arguments:
- embeddings: bfloat16 [163840, 1024], P(('gx', 'gy')), may hold values from -6 to 6
- device_local_selections: int32 [32, 64], P(('gx', 'gy')), may hold values from 0 to 5119
- merge_picks: int32 [32, 64], replicated, may hold values from 0 to 127
Outputs:
- final_centers: bfloat16 [64, 1024], replicated
- coverage: float32 [163840], P(('gx', 'gy'))
- radius: float32 [], replicated
All inputs are finite; a program needn't handle non-finite values.
Results may differ from a plain program's by a relative error of at most 0.001.
Values may be sent and summed in bfloat16 or wider, within the bound.
No kernel may reach another device: no remote copies, remote signals or barrier semaphores. Data moves between devices by JAX's collectives and lax.ppermute only.
A program may use at most 64 MiB of HBM per device.

v0:
```python
import functools

import jax
import jax.numpy as jnp
from jax import lax
from jax.experimental import pallas as pl
from jax.experimental.pallas import tpu as pltpu
from jax.sharding import PartitionSpec as P


GROUP = 8
LEGS = {"gy": ("south", "north", "shared"), "gx": ('south', 'shared', 'north')}
CHUNK = 256
NT = (((1,), (1,)), ((), ()))
VMEM = pl.BlockSpec(memory_space=pltpu.VMEM)


def cost(flops):
    return pl.CostEstimate(flops=flops, bytes_accessed=2**20, transcendentals=0)


def gather_kernel(picks_ref, points_ref, out_ref, held, sem):
    count = out_ref.shape[0]
    picks = [picks_ref[0, i] for i in range(count)]
    for i, pick in enumerate(picks):
        start = pl.multiple_of(lax.shift_right_logical(pick, 3) * GROUP, GROUP)
        pltpu.make_async_copy(
            points_ref.at[pl.ds(start, GROUP), :], held.at[pl.ds(i * GROUP, GROUP), :], sem
        ).start()
    down = lax.broadcasted_iota(jnp.int32, (count, 128), 0)
    wanted = down * GROUP
    for i, pick in enumerate(picks):
        wanted = jnp.where(down == i, wanted + (pick & (GROUP - 1)), wanted)
    lanes = lax.broadcasted_iota(jnp.int32, (count, 128), 1)
    onehot = jnp.concatenate(
        [(lanes + base == wanted).astype(jnp.bfloat16) for base in range(0, count * GROUP, 128)],
        axis=1,
    )
    pltpu.make_async_copy(points_ref.at[pl.ds(0, count * GROUP), :], held, sem).wait()
    out_ref[...] = jnp.dot(
        onehot, held[...], preferred_element_type=jnp.float32
    ).astype(jnp.bfloat16)


def gather_rows(points, picks):
    count = picks.shape[1]
    width = points.shape[1]
    return pl.pallas_call(
        gather_kernel,
        out_shape=pltpu.VMEM((count, width), points.dtype),
        in_specs=[
            pl.BlockSpec(memory_space=pltpu.SMEM),
            pl.BlockSpec(memory_space=pltpu.HBM),
        ],
        out_specs=VMEM,
        scratch_shapes=[
            pltpu.VMEM((count * GROUP, width), points.dtype),
            pltpu.SemaphoreType.DMA,
        ],
        compiler_params=pltpu.CompilerParams(vmem_limit_bytes=56 * 2**20),
        cost_estimate=cost(10**9),
        name="gather_rows",
    )(picks, points)


def swap_halves(index, count, lower):
    swapped_index = jnp.where(index < count, index + count, index - count)
    return jnp.where(lower, index, swapped_index)


def upright(row):
    size = row.shape[1]
    across = lax.broadcasted_iota(jnp.int32, (size, size), 1)
    down = lax.broadcasted_iota(jnp.int32, (size, size), 0)
    spread = jnp.where(across == down, jnp.broadcast_to(row, (size, size)), 0)
    return jnp.sum(spread.astype(jnp.float32), axis=1, keepdims=True).astype(jnp.int32)


def plan_kernel(phases, count, devices, picks_ref, *out_refs):
    number = lax.axis_index("gx") * lax.axis_size("gy") + lax.axis_index("gy")
    outs = list(out_refs)
    north = (number & 1) == 1

    def row_of(step, place):
        return picks_ref[pl.ds(devices - (devices >> step) + (place >> step + 1), 1), :]

    def onehot(column, total):
        lanes = lax.broadcasted_iota(jnp.int32, (column.shape[0], total), 1)
        return (lanes == column).astype(jnp.bfloat16)

    for step, kind in phases:
        lower = (number >> step & 1) == 0
        own = swap_halves(row_of(step, number), count, lower)
        if kind == "single":
            outs.pop(0)[...] = onehot(upright(own), 2 * count)
            continue
        beside = swap_halves(row_of(step, number ^ 2 << step), count, lower)
        lower_next = (number >> step + 1 & 1) == 0
        top = upright(swap_halves(row_of(step + 1, number), count, lower_next))
        lanes = lax.broadcasted_iota(jnp.int32, (count, count), 1)
        relative = jnp.where(lanes == top, own, 0) + jnp.where(
            lanes + count == top, beside + 2 * count, 0
        )
        relative = jnp.sum(relative.astype(jnp.float32), axis=1, keepdims=True)
        relative = relative.astype(jnp.int32)
        half = count // 2
        roles = [1 + LEGS[kind].index(role) for role in ("north", "south", "shared")]

        def placed(relative):
            place = relative
            for role, part, start_north, start_south in (
                (roles[0], None, count, count + 3 * half),
                (roles[1], None, count + 3 * half, count),
                (roles[2], 0, 2 * count, 2 * count + 3 * half),
                (roles[2], 1, 2 * count + 3 * half, 2 * count),
            ):
                base = role * count + (part or 0) * half
                extent = count if part is None else half
                inside = (relative >= base) & (relative < base + extent)
                start = jnp.where(north, start_north, start_south)
                place = jnp.where(inside, relative - base + start, place)
            return place

        outs.pop(0)[...] = onehot(placed(relative), 4 * count)
        plain = lax.broadcasted_iota(jnp.int32, (count, 1), 0) + count
        scored = jnp.concatenate([plain, upright(beside) + 2 * count], 0)
        outs.pop(0)[...] = onehot(placed(scored) - count, 3 * count)


def make_plan(picks, phases, devices):
    count = picks.shape[1]
    shapes = []
    for _, kind in phases:
        if kind == "single":
            shapes.append(pltpu.VMEM((count, 2 * count), jnp.bfloat16))
        else:
            shapes.append(pltpu.VMEM((count, 4 * count), jnp.bfloat16))
            shapes.append(pltpu.VMEM((2 * count, 3 * count), jnp.bfloat16))
    return pl.pallas_call(
        functools.partial(plan_kernel, phases, count, devices),
        out_shape=tuple(shapes),
        in_specs=[VMEM],
        out_specs=(VMEM,) * len(shapes),
        compiler_params=pltpu.CompilerParams(vmem_limit_bytes=4 * 2**20),
        cost_estimate=pl.CostEstimate(flops=10**10, bytes_accessed=2**27, transcendentals=0),
        name="plan",
    )(picks)


def prepare_kernel(points_ref, turned_ref, squares_ref):
    rows, width = points_ref.shape
    ones = jnp.ones((8, 128), jnp.bfloat16)
    down = lax.broadcasted_iota(jnp.int32, (CHUNK, CHUNK), 0)
    across = lax.broadcasted_iota(jnp.int32, (CHUNK, CHUNK), 1)
    identity = (down == across).astype(jnp.bfloat16)
    for piece in range(rows // CHUNK):
        window = pl.ds(piece * CHUNK, CHUNK)
        partial = None
        for lane in range(0, width, CHUNK):
            value = points_ref[window, pl.ds(lane, CHUNK)]
            turned_ref[pl.ds(lane, CHUNK), window] = lax.dot_general(
                identity, value, NT, preferred_element_type=jnp.float32
            ).astype(jnp.bfloat16)
            block = value.astype(jnp.float32)
            block = block * block
            for offset in range(0, CHUNK, 128):
                term = block[:, offset : offset + 128]
                partial = term if partial is None else partial + term
        high = partial.astype(jnp.bfloat16)
        low = (partial - high.astype(jnp.float32)).astype(jnp.bfloat16)
        total = lax.dot_general(
            ones, high, NT, preferred_element_type=jnp.float32
        ) + lax.dot_general(ones, low, NT, preferred_element_type=jnp.float32)
        squares_ref[:, window] = total[:1, :]


def prepare(points):
    rows, width = points.shape
    return pl.pallas_call(
        prepare_kernel,
        out_shape=(
            pltpu.VMEM((width, rows), points.dtype),
            pltpu.VMEM((1, rows), jnp.float32),
        ),
        in_specs=[VMEM],
        out_specs=(VMEM, VMEM),
        compiler_params=pltpu.CompilerParams(vmem_limit_bytes=16 * 2**20),
        cost_estimate=cost(3 * 10**9),
        name="prepare",
    )(points)


def score_kernel(shape, first, last, turned_ref, *refs):
    width, rows = turned_ref.shape
    refs = list(refs)
    values = []
    raw = []
    for chosen, number in shape:
        onehot = refs.pop(0)[...] if chosen else None
        raw.append([refs.pop(0) for _ in range(number)])
        value = jnp.concatenate([ref[...] for ref in raw[-1]], 0)
        if chosen:
            value = jnp.dot(onehot, value, preferred_element_type=jnp.float32)
            value = value.astype(jnp.bfloat16)
        values.append(value)
    value = values[0] if len(values) == 1 else jnp.concatenate(values, 0)
    wide = value.astype(jnp.float32)
    top = jnp.sum(wide * wide, axis=1, keepdims=True)
    weight = value * jnp.bfloat16(-2.0)
    before_ref = None if first else refs.pop(0)
    squares_ref = refs.pop(0) if last else None
    if last:
        onehot_ref, own_ref, out_ref, sets_ref, peak_ref = refs
        held = jnp.concatenate([own_ref[...]] + [ref[...] for ref in raw[-1]], 0)
        sets_ref[...] = jnp.dot(
            onehot_ref[...], held, preferred_element_type=jnp.float32
        ).astype(jnp.bfloat16)
    else:
        out_ref = refs.pop(0)
    peak = None
    for piece in range(rows // CHUNK):
        window = pl.ds(piece * CHUNK, CHUNK)
        part = jnp.dot(weight, turned_ref[:, window], preferred_element_type=jnp.float32)
        least = jnp.min(part + top, axis=0, keepdims=True)
        if not first:
            least = jnp.minimum(least, before_ref[:, window])
        if last:
            least = (least + squares_ref[:, window]) / width
            peak = least if peak is None else jnp.maximum(peak, least)
        out_ref[:, window] = least
    if last:
        most = jnp.max(peak, axis=1, keepdims=True)
        peak_ref[...] = jnp.broadcast_to(most[None], peak_ref.shape)


def score(turned, pending, before=None, squares=None, final=None, devices=0):
    _, rows = turned.shape
    operands = [turned]
    shape = []
    for onehot, sets in pending:
        shape.append((onehot is not None, len(sets)))
        operands += ([] if onehot is None else [onehot]) + list(sets)
    if before is not None:
        operands.append(before)
    last = final is not None
    out_shape = [pltpu.VMEM((1, rows), jnp.float32)]
    if last:
        operands += [squares, *final]
        out_shape += [
            pltpu.VMEM(final[1].shape, turned.dtype),
            pltpu.VMEM((devices, 1, 128), jnp.float32),
        ]
    return pl.pallas_call(
        functools.partial(score_kernel, tuple(shape), before is None, last),
        out_shape=tuple(out_shape),
        in_specs=[VMEM] * len(operands),
        out_specs=(VMEM,) * len(out_shape),
        compiler_params=pltpu.CompilerParams(vmem_limit_bytes=16 * 2**20),
        cost_estimate=cost(3 * 10**9),
        name="score_last" if last else "score",
    )(*operands)


def finish_kernel(peaks_ref, cover_ref, sets_ref, cover_out, sets_out, radius_out, radius, sems):
    radius[...] = jnp.max(jnp.max(peaks_ref[...], axis=0), axis=1, keepdims=True)
    copies = [
        pltpu.make_async_copy(source, target, sems.at[place])
        for place, (source, target) in enumerate(
            ((cover_ref, cover_out), (sets_ref, sets_out), (radius, radius_out))
        )
    ]
    for copy in copies:
        copy.start()
    for copy in copies:
        copy.wait()


def finish(peaks, cover, sets):
    hbm = pl.BlockSpec(memory_space=pltpu.HBM)
    return pl.pallas_call(
        finish_kernel,
        out_shape=(
            jax.ShapeDtypeStruct(cover.shape, cover.dtype),
            jax.ShapeDtypeStruct(sets.shape, sets.dtype),
            jax.ShapeDtypeStruct((1, 1), jnp.float32),
        ),
        in_specs=[VMEM] * 3,
        out_specs=(hbm, hbm, hbm),
        scratch_shapes=[pltpu.VMEM((1, 1), jnp.float32), pltpu.SemaphoreType.DMA((3,))],
        compiler_params=pltpu.CompilerParams(vmem_limit_bytes=4 * 2**20),
        name="finish",
    )(peaks, cover, sets)


def choose(onehot, held):
    rows = held[0] if len(held) == 1 else jnp.concatenate(held, 0)
    return jnp.dot(onehot, rows, preferred_element_type=jnp.float32).astype(rows.dtype)


def phase_spans(size_gx, size_gy):
    bits_gy = size_gy.bit_length() - 1
    rounds = bits_gy + size_gx.bit_length() - 1
    spans = [(0, 1)]
    for begin, end in ((1, bits_gy), (bits_gy, rounds)):
        for step in range(begin, end, 2):
            spans.append((step, min(step + 2, end)))
    return spans


def per_device(embeddings, device_local_selections, merge_picks):
    count = device_local_selections.shape[1]
    size_gx = lax.axis_size("gx")
    size_gy = lax.axis_size("gy")
    devices = size_gx * size_gy
    number = lax.axis_index("gx") * size_gy + lax.axis_index("gy")
    north = (number & 1) == 1

    def swap(value, mask, other=None):
        other = mask if other is None else other
        pairs = [(source, source ^ (mask if source & 1 else other)) for source in range(devices)]
        return lax.ppermute(value, ("gx", "gy"), pairs)

    phases = []
    for begin, end in phase_spans(size_gx, size_gy):
        kind = "gy" if end <= size_gy.bit_length() - 1 else "gx"
        phases.append((begin, kind if end - begin > 1 else "single"))

    sets = gather_rows(embeddings, device_local_selections)
    plan = list(make_plan(merge_picks, phases, devices))
    cover = None
    pending = []
    for place, (step, kind) in enumerate(phases):
        near, high = 1 << step, 2 << step
        onehot = plan.pop(0)
        if kind == "single":
            kept = None
            others = [swap(sets, near)]
        else:
            kept = plan.pop(0)
            masks = dict(zip(LEGS[kind], (near, high, near | high)))
            half = count // 2
            part = jnp.where(north, sets[:half], sets[half:])
            first = swap(sets, masks["north"], masks["south"])
            second = swap(part, masks["shared"])
            here = jnp.concatenate([first, second], 0)
            others = [here, swap(here, 1)]
        if place == 1:
            turned, squares = prepare(embeddings)
        elif place > 1:
            (cover,) = score(turned, pending, cover)
            pending = []
        pending.append((kept, ([sets] if step == 0 else []) + others))
        if place + 1 < len(phases):
            sets = choose(onehot, [sets] + others)
    cover, sets, peak = score(turned, pending, cover, squares, (onehot, sets), devices)
    peak = lax.all_to_all(peak, ("gx", "gy"), 0, 0, tiled=True)
    cover, sets, radius = finish(peak, cover, sets)
    return (sets, cover[0], radius[0, 0])


def solution(mesh):
    return jax.shard_map(
        per_device,
        mesh=mesh,
        in_specs=(P(("gx", "gy"), None), P(("gx", "gy"), None), P()),
        out_specs=(P(), P(("gx", "gy")), P()),
        check_vma=False,
    )
```

profile of v0, /device:TPU:0, one launch (start us, length us, event | category | flops | bytes accessed | tf_op | source)
XLA Modules:
  0.0 47.6 jit_solution(18146498635015599466)
XLA Ops:
  0.6 0.0 copy-start.1
  0.6 2.3 %gather_rows.1.refs_0_ = bf16[64,1024]{1,0:T(8,128)(2,1)S(1)} custom-call(s32[1,64]{1,0:T(1,128)} %picks_ref.3, bf16[5120,1024]{1,0:T(8,128)(2,1)} %points_ref.3), custom_call_target="tpu_custom_call" | custom-call | flops 1000000000 | bytes 1048576 | tf_op jit(solution)/shard_map/gather_rows/pallas_call | solution.py:48
  2.9 0.6 %collective-permute-start = (bf16[64,1024]{1,0:T(8,128)(2,1)S(1)}, bf16[64,1024]{1,0:T(8,128)(2,1)S(1)}, u32[]{:S(2)}, u32[]{:S(2)}) collective-permute-start(bf16[64,1024]{1,0:T(8,128)(2,1)S(1)} %gather_rows.1.refs_0_), channel_id=1, source_target_pairs={{0,1},{1,0},{2,3},{3,2},{4,5},{5,4},{6,7},{7,6},{8,9},{9,8},{10,11... | collective-permute-start | bytes 393224 | tf_op jit(solution)/shard_map/ppermute | solution.py:321
  3.5 0.0 copy-done.1
  3.5 0.3 plan.1
  3.8 0.7 %collective-permute-done.refs_1_ = bf16[64,1024]{1,0:T(8,128)(2,1)S(1)} collective-permute-done((bf16[64,1024]{1,0:T(8,128)(2,1)S(1)}, bf16[64,1024]{1,0:T(8,128)(2,1)S(1)}, u32[]{:S(2)}, u32[]{:S(2)}) %collective-permute-start) | collective-permute-done | bytes 131104 | tf_op jit(solution)/shard_map/ppermute | solution.py:321
  4.5 0.2 fusion.1
  4.7 3.0 %collective-permute-start.1 = (bf16[64,1024]{1,0:T(8,128)(2,1)S(1)}, bf16[64,1024]{1,0:T(8,128)(2,1)S(1)}, u32[]{:S(2)}, u32[]{:S(2)}) collective-permute-start(bf16[64,1024]{1,0:T(8,128)(2,1)S(1)} %fusion.1), channel_id=1, source_target_pairs={{0,2},{1,5},{2,0},{3,7},{4,6},{5,1},{6,4},{7,3},{8,10},{9,13},{10,... | collective-permute-start | bytes 393224 | tf_op jit(solution)/shard_map/ppermute | solution.py:321
  7.7 2.5 %collective-permute-start.2 = (bf16[32,1024]{1,0:T(8,128)(2,1)S(1)}, bf16[32,1024]{1,0:T(8,128)(2,1)S(1)}, u32[]{:S(2)}, u32[]{:S(2)}) collective-permute-start(bf16[32,1024]{1,0:T(8,128)(2,1)S(1)} %slice_select_fusion.1), channel_id=1, source_target_pairs={{0,6},{1,7},{2,4},{3,5},{4,2},{5,3},{6,0},{7,1},{8,14},{9,15},{10,... | collective-permute-start | bytes 196616 | tf_op jit(solution)/shard_map/ppermute | solution.py:321
  10.2 1.5 %collective-permute-done.1 = bf16[64,1024]{1,0:T(8,128)(2,1)S(1)} collective-permute-done((bf16[64,1024]{1,0:T(8,128)(2,1)S(1)}, bf16[64,1024]{1,0:T(8,128)(2,1)S(1)}, u32[]{:S(2)}, u32[]{:S(2)}) %collective-permute-start.1) | collective-permute-done | bytes 131104 | tf_op jit(solution)/shard_map/ppermute | solution.py:321
  11.7 3.2 %collective-permute-done.2 = bf16[32,1024]{1,0:T(8,128)(2,1)S(1)} collective-permute-done((bf16[32,1024]{1,0:T(8,128)(2,1)S(1)}, bf16[32,1024]{1,0:T(8,128)(2,1)S(1)}, u32[]{:S(2)}, u32[]{:S(2)}) %collective-permute-start.2) | collective-permute-done | bytes 65568 | tf_op jit(solution)/shard_map/ppermute | solution.py:321
  15.0 0.0 collective-permute-start.3
  15.0 0.0 copy-start
  15.0 4.0 %copy-done = bf16[5120,1024]{1,0:T(8,128)(2,1)S(1)} copy-done((bf16[5120,1024]{1,0:T(8,128)(2,1)S(1)}, bf16[5120,1024]{1,0:T(8,128)(2,1)}, u32[]{:S(2)}) %copy-start) | copy-done | bytes 10485784
  18.9 4.2 %prepare.1 = (bf16[1024,5120]{1,0:T(8,128)(2,1)S(1)}, f32[1,5120]{1,0:T(1,128)S(1)}) custom-call(bf16[5120,1024]{1,0:T(8,128)(2,1)S(1)} %copy-done), custom_call_target="tpu_custom_call" | custom-call | flops 3000000000 | bytes 1048576 | tf_op jit(solution)/shard_map/prepare/pallas_call | solution.py:179
  23.1 0.0 collective-permute-done.3.refs_4_
  23.1 0.2 fusion.refs_6_
  23.3 1.6 %collective-permute-start.4 = (bf16[64,1024]{1,0:T(8,128)(2,1)S(1)}, bf16[64,1024]{1,0:T(8,128)(2,1)S(1)}, u32[]{:S(2)}, u32[]{:S(2)}) collective-permute-start(bf16[64,1024]{1,0:T(8,128)(2,1)S(1)} %fusion.refs_6_), channel_id=1, source_target_pairs={{0,8},{1,25},{2,10},{3,27},{4,12},{5,29},{6,14},{7,31},{8,0},{9,17... | collective-permute-start | bytes 393224 | tf_op jit(solution)/shard_map/ppermute | solution.py:321
  24.9 1.6 %collective-permute-start.5 = (bf16[32,1024]{1,0:T(8,128)(2,1)S(1)}, bf16[32,1024]{1,0:T(8,128)(2,1)S(1)}, u32[]{:S(2)}, u32[]{:S(2)}) collective-permute-start(bf16[32,1024]{1,0:T(8,128)(2,1)S(1)} %slice_select_fusion), channel_id=1, source_target_pairs={{0,16},{1,17},{2,18},{3,19},{4,20},{5,21},{6,22},{7,23},{8,24},{9,... | collective-permute-start | bytes 196616 | tf_op jit(solution)/shard_map/ppermute | solution.py:321
  26.5 2.8 %collective-permute-done.4 = bf16[64,1024]{1,0:T(8,128)(2,1)S(1)} collective-permute-done((bf16[64,1024]{1,0:T(8,128)(2,1)S(1)}, bf16[64,1024]{1,0:T(8,128)(2,1)S(1)}, u32[]{:S(2)}, u32[]{:S(2)}) %collective-permute-start.4) | collective-permute-done | bytes 131104 | tf_op jit(solution)/shard_map/ppermute | solution.py:321
  29.3 1.1 %collective-permute-done.5 = bf16[32,1024]{1,0:T(8,128)(2,1)S(1)} collective-permute-done((bf16[32,1024]{1,0:T(8,128)(2,1)S(1)}, bf16[32,1024]{1,0:T(8,128)(2,1)S(1)}, u32[]{:S(2)}, u32[]{:S(2)}) %collective-permute-start.5) | collective-permute-done | bytes 65568 | tf_op jit(solution)/shard_map/ppermute | solution.py:321
  30.4 0.1 collective-permute-start.6
  30.5 3.0 %score.1.refs_3_ = f32[1,5120]{1,0:T(1,128)S(1)} custom-call(bf16[1024,5120]{1,0:T(8,128)(2,1)S(1)} %get-tuple-element.16.turned_ref, bf16[64,1024]{1,0:T(8,128)(2,1)S(1)} %gather_rows.1.refs_0_, bf16[64,1024]{1,0:T(8,128)(2,1)S(1)} %collective-permute-done.refs_1_, bf16[128,192]{1,0:T(8,128)(2,1)S(1)} %get-tuple-element.20.refs_2_, ...), custom_call_target="tpu_custom_call" | custom-call | flops 3000000000 | bytes 1048576 | tf_op jit(solution)/shard_map/score/pallas_call | solution.py:253
  33.6 0.0 collective-permute-done.6.refs_2_
  33.6 1.9 %score_last.1 = (f32[1,5120]{1,0:T(1,128)S(1)}, bf16[64,1024]{1,0:T(8,128)(2,1)S(1)}, f32[32,1,128]{2,1,0:T(1,128)S(1)}) custom-call(bf16[1024,5120]{1,0:T(8,128)(2,1)S(1)} %get-tuple-element.16.turned_ref, bf16[128,192]{1,0:T(8,128)(2,1)S(1)} %get-tuple-element.17.refs_0_, bf16[96,1024]{1,0:T(8,128)(2,1)S(1)} %constant_dynamic-update-slice_fusion.2.refs_1_, ...), custom_call_target="tpu_custom_call" | custom-call | flops 3000000000 | bytes 1048576 | tf_op jit(solution)/shard_map/score_last/pallas_call | solution.py:253
  35.4 11.4 %all_to_all.5.peaks_ref = f32[32,1,128]{2,1,0:T(1,128)S(1)} all-to-all(f32[32,1,128]{2,1,0:T(1,128)S(1)} %get-tuple-element.23), channel_id=1, replica_groups=mesh['gx'=4,'gy'=8] {'gx','gy'}, dimensions={0} | all-to-all | bytes 32768 | tf_op jit(solution)/shard_map/all_to_all | solution.py:356
  46.9 0.7 %finish.1 = (f32[1,5120]{1,0:T(1,128)}, bf16[64,1024]{1,0:T(8,128)(2,1)}, f32[1,1]{1,0:T(1,128)}) custom-call(f32[32,1,128]{2,1,0:T(1,128)S(1)} %all_to_all.5.peaks_ref, f32[1,5120]{1,0:T(1,128)S(1)} %get-tuple-element.24.cover_ref, bf16[64,1024]{1,0:T(8,128)(2,1)S(1)} %get-tuple-element.25.sets_ref), custom_call_target="tpu_custom_call" | custom-call | tf_op jit(solution)/shard_map/finish/pallas_call | solution.py:280
  (6 shorter events, 0.0 us)
Async XLA Ops:
  0.6 2.9 %copy-start.1 = (s32[32,64]{1,0:T(8,128)S(1)}, s32[32,64]{1,0:T(8,128)}, u32[]{:S(2)}) copy-start(s32[32,64]{1,0:T(8,128)} %picks_ref.2) | copy-start | bytes 24580
  2.9 1.5 %collective-permute-start = (bf16[64,1024]{1,0:T(8,128)(2,1)S(1)}, bf16[64,1024]{1,0:T(8,128)(2,1)S(1)}, u32[]{:S(2)}, u32[]{:S(2)}) collective-permute-start(bf16[64,1024]{1,0:T(8,128)(2,1)S(1)} %gather_rows.1.refs_0_), channel_id=1, source_target_pairs={{0,1},{1,0},{2,3},{3,2},{4,5},{5,4},{6,7},{7,6},{8,9},{9,8},{10,11... | collective-permute-start | bytes 393224 | tf_op jit(solution)/shard_map/ppermute | solution.py:321
  4.7 7.1 %collective-permute-start.1 = (bf16[64,1024]{1,0:T(8,128)(2,1)S(1)}, bf16[64,1024]{1,0:T(8,128)(2,1)S(1)}, u32[]{:S(2)}, u32[]{:S(2)}) collective-permute-start(bf16[64,1024]{1,0:T(8,128)(2,1)S(1)} %fusion.1), channel_id=1, source_target_pairs={{0,2},{1,5},{2,0},{3,7},{4,6},{5,1},{6,4},{7,3},{8,10},{9,13},{10,... | collective-permute-start | bytes 393224 | tf_op jit(solution)/shard_map/ppermute | solution.py:321
  7.7 7.3 %collective-permute-start.2 = (bf16[32,1024]{1,0:T(8,128)(2,1)S(1)}, bf16[32,1024]{1,0:T(8,128)(2,1)S(1)}, u32[]{:S(2)}, u32[]{:S(2)}) collective-permute-start(bf16[32,1024]{1,0:T(8,128)(2,1)S(1)} %slice_select_fusion.1), channel_id=1, source_target_pairs={{0,6},{1,7},{2,4},{3,5},{4,2},{5,3},{6,0},{7,1},{8,14},{9,15},{10,... | collective-permute-start | bytes 196616 | tf_op jit(solution)/shard_map/ppermute | solution.py:321
  15.0 8.2 %collective-permute-start.3 = (bf16[96,1024]{1,0:T(8,128)(2,1)S(1)}, bf16[96,1024]{1,0:T(8,128)(2,1)S(1)}, u32[]{:S(2)}, u32[]{:S(2)}) collective-permute-start(bf16[96,1024]{1,0:T(8,128)(2,1)S(1)} %constant_dynamic-update-slice_fusion.refs_3_), channel_id=1, source_target_pairs={{0,1},{1,0},{2,3},{3,2},{4,5},{5,4},{6,7},{7,6},{8,9},{9,8},{10,11... | collective-permute-start | bytes 589832 | tf_op jit(solution)/shard_map/ppermute | solution.py:321
  15.0 4.0 %copy-start = (bf16[5120,1024]{1,0:T(8,128)(2,1)S(1)}, bf16[5120,1024]{1,0:T(8,128)(2,1)}, u32[]{:S(2)}) copy-start(bf16[5120,1024]{1,0:T(8,128)(2,1)} %points_ref.3) | copy-start | bytes 31457284
  23.3 5.9 %collective-permute-start.4 = (bf16[64,1024]{1,0:T(8,128)(2,1)S(1)}, bf16[64,1024]{1,0:T(8,128)(2,1)S(1)}, u32[]{:S(2)}, u32[]{:S(2)}) collective-permute-start(bf16[64,1024]{1,0:T(8,128)(2,1)S(1)} %fusion.refs_6_), channel_id=1, source_target_pairs={{0,8},{1,25},{2,10},{3,27},{4,12},{5,29},{6,14},{7,31},{8,0},{9,17... | collective-permute-start | bytes 393224 | tf_op jit(solution)/shard_map/ppermute | solution.py:321
  24.9 5.5 %collective-permute-start.5 = (bf16[32,1024]{1,0:T(8,128)(2,1)S(1)}, bf16[32,1024]{1,0:T(8,128)(2,1)S(1)}, u32[]{:S(2)}, u32[]{:S(2)}) collective-permute-start(bf16[32,1024]{1,0:T(8,128)(2,1)S(1)} %slice_select_fusion), channel_id=1, source_target_pairs={{0,16},{1,17},{2,18},{3,19},{4,20},{5,21},{6,22},{7,23},{8,24},{9,... | collective-permute-start | bytes 196616 | tf_op jit(solution)/shard_map/ppermute | solution.py:321
  30.4 3.2 %collective-permute-start.6 = (bf16[96,1024]{1,0:T(8,128)(2,1)S(1)}, bf16[96,1024]{1,0:T(8,128)(2,1)S(1)}, u32[]{:S(2)}, u32[]{:S(2)}) collective-permute-start(bf16[96,1024]{1,0:T(8,128)(2,1)S(1)} %constant_dynamic-update-slice_fusion.2.refs_1_), channel_id=1, source_target_pairs={{0,1},{1,0},{2,3},{3,2},{4,5},{5,4},{6,7},{7,6},{8,9},{9,8},{10,11... | collective-permute-start | bytes 589832 | tf_op jit(solution)/shard_map/ppermute | solution.py:321
where the time goes:
time: 47.9 us; the launch traced here: 47.6 us
  Pallas kernels  12.3 us (26%)
  blocking collectives  11.4 us (24%)
  starting transfers between devices  9.34 us (19%)
  waiting for transfers between devices  9.32 us (19%)
  local copies, waits for them, and re-layouts  4.01 us (8%)
  between operations  0.74 us (2%)
    all_to_all x1, blocking collectives, per_device(): peak = lax.all_to_all(peak, ('gx', 'gy'), 0, 0, tiled=True)  11.4 us
    ppermute x7, starting transfers between devices, swap(): return lax.ppermute(value, ('gx', 'gy'), pairs)  9.34 us
    ppermute x7, waiting for transfers between devices, swap(): return lax.ppermute(value, ('gx', 'gy'), pairs)  9.32 us
    pallas_call x2, Pallas kernels, score(): pl.pallas_call(functools.partial(score_kernel, tuple(shape), before is No...  4.9 us
    pallas_call x1, Pallas kernels, prepare(): pl.pallas_call(prepare_kernel, out_shape=(pltpu.VMEM((width, rows), point...  4.17 us
    unnamed x6, local copies, waits for them, and re-layouts  4 us
    pallas_call x1, Pallas kernels, gather_rows(): pl.pallas_call(gather_kernel, out_shape=pltpu.VMEM((count, width), points...  2.29 us
  transfers between devices with their start and end apart: 7, of which 5 were waited for; matrix products, arithmetic and copies ran while one was open for 0% of the time, Pallas kernels for 16%

commit v1 on v0

--- a/solution.py
+++ b/solution.py
@@ -210,7 +210,8 @@
     before_ref = None if first else refs.pop(0)
     squares_ref = refs.pop(0) if last else None
     if last:
-        onehot_ref, own_ref, out_ref, sets_ref, peak_ref = refs
+        onehot_ref, own_ref, out_ref, sets_out, peak_ref, sets_ref, sem = refs
+        sets_copy = pltpu.make_async_copy(sets_ref, sets_out, sem)
         held = jnp.concatenate([own_ref[...]] + [ref[...] for ref in raw[-1]], 0)
         sets_ref[...] = jnp.dot(
             onehot_ref[...], held, preferred_element_type=jnp.float32
@@ -228,7 +229,10 @@
             least = (least + squares_ref[:, window]) / width
             peak = least if peak is None else jnp.maximum(peak, least)
         out_ref[:, window] = least
+        if last and piece == 1:
+            sets_copy.start()
     if last:
+        sets_copy.wait()
         most = jnp.max(peak, axis=1, keepdims=True)
         peak_ref[...] = jnp.broadcast_to(most[None], peak_ref.shape)
 
@@ -247,26 +251,29 @@
     if last:
         operands += [squares, *final]
         out_shape += [
-            pltpu.VMEM(final[1].shape, turned.dtype),
+            jax.ShapeDtypeStruct(final[1].shape, turned.dtype),
             pltpu.VMEM((devices, 1, 128), jnp.float32),
         ]
     return pl.pallas_call(
         functools.partial(score_kernel, tuple(shape), before is None, last),
         out_shape=tuple(out_shape),
         in_specs=[VMEM] * len(operands),
-        out_specs=(VMEM,) * len(out_shape),
+        out_specs=(VMEM, pl.BlockSpec(memory_space=pltpu.HBM), VMEM) if last else (VMEM,),
+        scratch_shapes=[pltpu.VMEM(final[1].shape, turned.dtype), pltpu.SemaphoreType.DMA]
+        if last
+        else [],
         compiler_params=pltpu.CompilerParams(vmem_limit_bytes=16 * 2**20),
         cost_estimate=cost(3 * 10**9),
         name="score_last" if last else "score",
     )(*operands)
 
 
-def finish_kernel(peaks_ref, cover_ref, sets_ref, cover_out, sets_out, radius_out, radius, sems):
+def finish_kernel(peaks_ref, cover_ref, cover_out, radius_out, radius, sems):
     radius[...] = jnp.max(jnp.max(peaks_ref[...], axis=0), axis=1, keepdims=True)
     copies = [
         pltpu.make_async_copy(source, target, sems.at[place])
         for place, (source, target) in enumerate(
-            ((cover_ref, cover_out), (sets_ref, sets_out), (radius, radius_out))
+            ((cover_ref, cover_out), (radius, radius_out))
         )
     ]
     for copy in copies:
@@ -275,21 +282,20 @@
         copy.wait()
 
 
-def finish(peaks, cover, sets):
+def finish(peaks, cover):
     hbm = pl.BlockSpec(memory_space=pltpu.HBM)
     return pl.pallas_call(
         finish_kernel,
         out_shape=(
             jax.ShapeDtypeStruct(cover.shape, cover.dtype),
-            jax.ShapeDtypeStruct(sets.shape, sets.dtype),
             jax.ShapeDtypeStruct((1, 1), jnp.float32),
         ),
-        in_specs=[VMEM] * 3,
-        out_specs=(hbm, hbm, hbm),
-        scratch_shapes=[pltpu.VMEM((1, 1), jnp.float32), pltpu.SemaphoreType.DMA((3,))],
+        in_specs=[VMEM] * 2,
+        out_specs=(hbm, hbm),
+        scratch_shapes=[pltpu.VMEM((1, 1), jnp.float32), pltpu.SemaphoreType.DMA((2,))],
         compiler_params=pltpu.CompilerParams(vmem_limit_bytes=4 * 2**20),
         name="finish",
-    )(peaks, cover, sets)
+    )(peaks, cover)
 
 
 def choose(onehot, held):
@@ -354,7 +360,7 @@
             sets = choose(onehot, [sets] + others)
     cover, sets, peak = score(turned, pending, cover, squares, (onehot, sets), devices)
     peak = lax.all_to_all(peak, ("gx", "gy"), 0, 0, tiled=True)
-    cover, sets, radius = finish(peak, cover, sets)
+    cover, radius = finish(peak, cover)
     return (sets, cover[0], radius[0, 0])
 
 

time: 47.9 us -> 47.9 us (level)
  no operation moved by 1% of the time
where the time goes in v1:
time: 47.9 us; the launch traced here: 47.6 us
  Pallas kernels  12.3 us (26%)
  blocking collectives  11.4 us (24%)
  starting transfers between devices  9.34 us (19%)
  waiting for transfers between devices  9.32 us (19%)
  local copies, waits for them, and re-layouts  4.01 us (8%)
  between operations  0.75 us (2%)
    all_to_all x1, blocking collectives, per_device(): peak = lax.all_to_all(peak, ('gx', 'gy'), 0, 0, tiled=True)  11.4 us
    ppermute x7, starting transfers between devices, swap(): return lax.ppermute(value, ('gx', 'gy'), pairs)  9.34 us
    ppermute x7, waiting for transfers between devices, swap(): return lax.ppermute(value, ('gx', 'gy'), pairs)  9.32 us
    pallas_call x2, Pallas kernels, score(): pl.pallas_call(functools.partial(score_kernel, tuple(shape), before is No...  4.94 us
    pallas_call x1, Pallas kernels, prepare(): pl.pallas_call(prepare_kernel, out_shape=(pltpu.VMEM((width, rows), point...  4.17 us
    unnamed x6, local copies, waits for them, and re-layouts  4 us
    pallas_call x1, Pallas kernels, gather_rows(): pl.pallas_call(gather_kernel, out_shape=pltpu.VMEM((count, width), points...  2.29 us
  transfers between devices with their start and end apart: 7, of which 5 were waited for; matrix products, arithmetic and copies ran while one was open for 0% of the time, Pallas kernels for 16%

profile of v1, /device:TPU:0, one launch (start us, length us, event | category | flops | bytes accessed | tf_op | source)
XLA Modules:
  0.0 47.6 jit_solution(10008219513761445982)
XLA Ops:
  0.6 0.0 copy-start.1
  0.6 2.3 %gather_rows.1.refs_0_ = bf16[64,1024]{1,0:T(8,128)(2,1)S(1)} custom-call(s32[1,64]{1,0:T(1,128)} %picks_ref.3, bf16[5120,1024]{1,0:T(8,128)(2,1)} %points_ref.3), custom_call_target="tpu_custom_call" | custom-call | flops 1000000000 | bytes 1048576 | tf_op jit(solution)/shard_map/gather_rows/pallas_call | solution.py:48
  2.9 0.6 %collective-permute-start = (bf16[64,1024]{1,0:T(8,128)(2,1)S(1)}, bf16[64,1024]{1,0:T(8,128)(2,1)S(1)}, u32[]{:S(2)}, u32[]{:S(2)}) collective-permute-start(bf16[64,1024]{1,0:T(8,128)(2,1)S(1)} %gather_rows.1.refs_0_), channel_id=1, source_target_pairs={{0,1},{1,0},{2,3},{3,2},{4,5},{5,4},{6,7},{7,6},{8,9},{9,8},{10,11... | collective-permute-start | bytes 393224 | tf_op jit(solution)/shard_map/ppermute | solution.py:327
  3.5 0.0 copy-done.1
  3.5 0.3 plan.1
  3.8 0.7 %collective-permute-done.refs_1_ = bf16[64,1024]{1,0:T(8,128)(2,1)S(1)} collective-permute-done((bf16[64,1024]{1,0:T(8,128)(2,1)S(1)}, bf16[64,1024]{1,0:T(8,128)(2,1)S(1)}, u32[]{:S(2)}, u32[]{:S(2)}) %collective-permute-start) | collective-permute-done | bytes 131104 | tf_op jit(solution)/shard_map/ppermute | solution.py:327
  4.5 0.2 fusion.1
  4.7 3.0 %collective-permute-start.1 = (bf16[64,1024]{1,0:T(8,128)(2,1)S(1)}, bf16[64,1024]{1,0:T(8,128)(2,1)S(1)}, u32[]{:S(2)}, u32[]{:S(2)}) collective-permute-start(bf16[64,1024]{1,0:T(8,128)(2,1)S(1)} %fusion.1), channel_id=1, source_target_pairs={{0,2},{1,5},{2,0},{3,7},{4,6},{5,1},{6,4},{7,3},{8,10},{9,13},{10,... | collective-permute-start | bytes 393224 | tf_op jit(solution)/shard_map/ppermute | solution.py:327
  7.7 2.5 %collective-permute-start.2 = (bf16[32,1024]{1,0:T(8,128)(2,1)S(1)}, bf16[32,1024]{1,0:T(8,128)(2,1)S(1)}, u32[]{:S(2)}, u32[]{:S(2)}) collective-permute-start(bf16[32,1024]{1,0:T(8,128)(2,1)S(1)} %slice_select_fusion.1), channel_id=1, source_target_pairs={{0,6},{1,7},{2,4},{3,5},{4,2},{5,3},{6,0},{7,1},{8,14},{9,15},{10,... | collective-permute-start | bytes 196616 | tf_op jit(solution)/shard_map/ppermute | solution.py:327
  10.2 1.5 %collective-permute-done.1 = bf16[64,1024]{1,0:T(8,128)(2,1)S(1)} collective-permute-done((bf16[64,1024]{1,0:T(8,128)(2,1)S(1)}, bf16[64,1024]{1,0:T(8,128)(2,1)S(1)}, u32[]{:S(2)}, u32[]{:S(2)}) %collective-permute-start.1) | collective-permute-done | bytes 131104 | tf_op jit(solution)/shard_map/ppermute | solution.py:327
  11.7 3.2 %collective-permute-done.2 = bf16[32,1024]{1,0:T(8,128)(2,1)S(1)} collective-permute-done((bf16[32,1024]{1,0:T(8,128)(2,1)S(1)}, bf16[32,1024]{1,0:T(8,128)(2,1)S(1)}, u32[]{:S(2)}, u32[]{:S(2)}) %collective-permute-start.2) | collective-permute-done | bytes 65568 | tf_op jit(solution)/shard_map/ppermute | solution.py:327
  15.0 0.0 collective-permute-start.3
  15.0 0.0 copy-start
  15.0 4.0 %copy-done = bf16[5120,1024]{1,0:T(8,128)(2,1)S(1)} copy-done((bf16[5120,1024]{1,0:T(8,128)(2,1)S(1)}, bf16[5120,1024]{1,0:T(8,128)(2,1)}, u32[]{:S(2)}) %copy-start) | copy-done | bytes 10485784
  18.9 4.2 %prepare.1 = (bf16[1024,5120]{1,0:T(8,128)(2,1)S(1)}, f32[1,5120]{1,0:T(1,128)S(1)}) custom-call(bf16[5120,1024]{1,0:T(8,128)(2,1)S(1)} %copy-done), custom_call_target="tpu_custom_call" | custom-call | flops 3000000000 | bytes 1048576 | tf_op jit(solution)/shard_map/prepare/pallas_call | solution.py:179
  23.1 0.0 collective-permute-done.3.refs_4_
  23.1 0.2 fusion.refs_6_
  23.3 1.6 %collective-permute-start.4 = (bf16[64,1024]{1,0:T(8,128)(2,1)S(1)}, bf16[64,1024]{1,0:T(8,128)(2,1)S(1)}, u32[]{:S(2)}, u32[]{:S(2)}) collective-permute-start(bf16[64,1024]{1,0:T(8,128)(2,1)S(1)} %fusion.refs_6_), channel_id=1, source_target_pairs={{0,8},{1,25},{2,10},{3,27},{4,12},{5,29},{6,14},{7,31},{8,0},{9,17... | collective-permute-start | bytes 393224 | tf_op jit(solution)/shard_map/ppermute | solution.py:327
  24.9 1.6 %collective-permute-start.5 = (bf16[32,1024]{1,0:T(8,128)(2,1)S(1)}, bf16[32,1024]{1,0:T(8,128)(2,1)S(1)}, u32[]{:S(2)}, u32[]{:S(2)}) collective-permute-start(bf16[32,1024]{1,0:T(8,128)(2,1)S(1)} %slice_select_fusion), channel_id=1, source_target_pairs={{0,16},{1,17},{2,18},{3,19},{4,20},{5,21},{6,22},{7,23},{8,24},{9,... | collective-permute-start | bytes 196616 | tf_op jit(solution)/shard_map/ppermute | solution.py:327
  26.5 2.8 %collective-permute-done.4 = bf16[64,1024]{1,0:T(8,128)(2,1)S(1)} collective-permute-done((bf16[64,1024]{1,0:T(8,128)(2,1)S(1)}, bf16[64,1024]{1,0:T(8,128)(2,1)S(1)}, u32[]{:S(2)}, u32[]{:S(2)}) %collective-permute-start.4) | collective-permute-done | bytes 131104 | tf_op jit(solution)/shard_map/ppermute | solution.py:327
  29.3 1.1 %collective-permute-done.5 = bf16[32,1024]{1,0:T(8,128)(2,1)S(1)} collective-permute-done((bf16[32,1024]{1,0:T(8,128)(2,1)S(1)}, bf16[32,1024]{1,0:T(8,128)(2,1)S(1)}, u32[]{:S(2)}, u32[]{:S(2)}) %collective-permute-start.5) | collective-permute-done | bytes 65568 | tf_op jit(solution)/shard_map/ppermute | solution.py:327
  30.4 0.1 collective-permute-start.6
  30.5 3.1 %score.1.refs_3_ = f32[1,5120]{1,0:T(1,128)S(1)} custom-call(bf16[1024,5120]{1,0:T(8,128)(2,1)S(1)} %get-tuple-element.15.turned_ref, bf16[64,1024]{1,0:T(8,128)(2,1)S(1)} %gather_rows.1.refs_0_, bf16[64,1024]{1,0:T(8,128)(2,1)S(1)} %collective-permute-done.refs_1_, bf16[128,192]{1,0:T(8,128)(2,1)S(1)} %get-tuple-element.19.refs_2_, ...), custom_call_target="tpu_custom_call" | custom-call | flops 3000000000 | bytes 1048576 | tf_op jit(solution)/shard_map/score/pallas_call | solution.py:257
  33.6 0.0 collective-permute-done.6.refs_2_
  33.6 1.9 %score_last.1 = (f32[1,5120]{1,0:T(1,128)S(1)}, bf16[64,1024]{1,0:T(8,128)(2,1)}, f32[32,1,128]{2,1,0:T(1,128)S(1)}) custom-call(bf16[1024,5120]{1,0:T(8,128)(2,1)S(1)} %get-tuple-element.15.turned_ref, bf16[128,192]{1,0:T(8,128)(2,1)S(1)} %get-tuple-element.16.refs_0_, bf16[96,1024]{1,0:T(8,128)(2,1)S(1)} %constant_dynamic-update-slice_fusion.2.refs_1_, ...), custom_call_target="tpu_custom_call" | custom-call | flops 3000000000 | bytes 1048576 | tf_op jit(solution)/shard_map/score_last/pallas_call | solution.py:257
  35.5 11.4 %all_to_all.5.peaks_ref = f32[32,1,128]{2,1,0:T(1,128)S(1)} all-to-all(f32[32,1,128]{2,1,0:T(1,128)S(1)} %get-tuple-element.23), channel_id=1, replica_groups=mesh['gx'=4,'gy'=8] {'gx','gy'}, dimensions={0} | all-to-all | bytes 32768 | tf_op jit(solution)/shard_map/all_to_all | solution.py:362
  46.9 0.6 %finish.1 = (f32[1,5120]{1,0:T(1,128)}, f32[1,1]{1,0:T(1,128)}) custom-call(f32[32,1,128]{2,1,0:T(1,128)S(1)} %all_to_all.5.peaks_ref, f32[1,5120]{1,0:T(1,128)S(1)} %get-tuple-element.24.cover_ref), custom_call_target="tpu_custom_call" | custom-call | tf_op jit(solution)/shard_map/finish/pallas_call | solution.py:287
  (6 shorter events, 0.0 us)
Async XLA Ops:
  0.6 2.9 %copy-start.1 = (s32[32,64]{1,0:T(8,128)S(1)}, s32[32,64]{1,0:T(8,128)}, u32[]{:S(2)}) copy-start(s32[32,64]{1,0:T(8,128)} %picks_ref.2) | copy-start | bytes 24580
  2.9 1.5 %collective-permute-start = (bf16[64,1024]{1,0:T(8,128)(2,1)S(1)}, bf16[64,1024]{1,0:T(8,128)(2,1)S(1)}, u32[]{:S(2)}, u32[]{:S(2)}) collective-permute-start(bf16[64,1024]{1,0:T(8,128)(2,1)S(1)} %gather_rows.1.refs_0_), channel_id=1, source_target_pairs={{0,1},{1,0},{2,3},{3,2},{4,5},{5,4},{6,7},{7,6},{8,9},{9,8},{10,11... | collective-permute-start | bytes 393224 | tf_op jit(solution)/shard_map/ppermute | solution.py:327
  4.7 7.1 %collective-permute-start.1 = (bf16[64,1024]{1,0:T(8,128)(2,1)S(1)}, bf16[64,1024]{1,0:T(8,128)(2,1)S(1)}, u32[]{:S(2)}, u32[]{:S(2)}) collective-permute-start(bf16[64,1024]{1,0:T(8,128)(2,1)S(1)} %fusion.1), channel_id=1, source_target_pairs={{0,2},{1,5},{2,0},{3,7},{4,6},{5,1},{6,4},{7,3},{8,10},{9,13},{10,... | collective-permute-start | bytes 393224 | tf_op jit(solution)/shard_map/ppermute | solution.py:327
  7.7 7.3 %collective-permute-start.2 = (bf16[32,1024]{1,0:T(8,128)(2,1)S(1)}, bf16[32,1024]{1,0:T(8,128)(2,1)S(1)}, u32[]{:S(2)}, u32[]{:S(2)}) collective-permute-start(bf16[32,1024]{1,0:T(8,128)(2,1)S(1)} %slice_select_fusion.1), channel_id=1, source_target_pairs={{0,6},{1,7},{2,4},{3,5},{4,2},{5,3},{6,0},{7,1},{8,14},{9,15},{10,... | collective-permute-start | bytes 196616 | tf_op jit(solution)/shard_map/ppermute | solution.py:327
  15.0 8.2 %collective-permute-start.3 = (bf16[96,1024]{1,0:T(8,128)(2,1)S(1)}, bf16[96,1024]{1,0:T(8,128)(2,1)S(1)}, u32[]{:S(2)}, u32[]{:S(2)}) collective-permute-start(bf16[96,1024]{1,0:T(8,128)(2,1)S(1)} %constant_dynamic-update-slice_fusion.refs_3_), channel_id=1, source_target_pairs={{0,1},{1,0},{2,3},{3,2},{4,5},{5,4},{6,7},{7,6},{8,9},{9,8},{10,11... | collective-permute-start | bytes 589832 | tf_op jit(solution)/shard_map/ppermute | solution.py:327
  15.0 4.0 %copy-start = (bf16[5120,1024]{1,0:T(8,128)(2,1)S(1)}, bf16[5120,1024]{1,0:T(8,128)(2,1)}, u32[]{:S(2)}) copy-start(bf16[5120,1024]{1,0:T(8,128)(2,1)} %points_ref.3) | copy-start | bytes 31457284
  23.3 5.9 %collective-permute-start.4 = (bf16[64,1024]{1,0:T(8,128)(2,1)S(1)}, bf16[64,1024]{1,0:T(8,128)(2,1)S(1)}, u32[]{:S(2)}, u32[]{:S(2)}) collective-permute-start(bf16[64,1024]{1,0:T(8,128)(2,1)S(1)} %fusion.refs_6_), channel_id=1, source_target_pairs={{0,8},{1,25},{2,10},{3,27},{4,12},{5,29},{6,14},{7,31},{8,0},{9,17... | collective-permute-start | bytes 393224 | tf_op jit(solution)/shard_map/ppermute | solution.py:327
  24.9 5.5 %collective-permute-start.5 = (bf16[32,1024]{1,0:T(8,128)(2,1)S(1)}, bf16[32,1024]{1,0:T(8,128)(2,1)S(1)}, u32[]{:S(2)}, u32[]{:S(2)}) collective-permute-start(bf16[32,1024]{1,0:T(8,128)(2,1)S(1)} %slice_select_fusion), channel_id=1, source_target_pairs={{0,16},{1,17},{2,18},{3,19},{4,20},{5,21},{6,22},{7,23},{8,24},{9,... | collective-permute-start | bytes 196616 | tf_op jit(solution)/shard_map/ppermute | solution.py:327
  30.4 3.2 %collective-permute-start.6 = (bf16[96,1024]{1,0:T(8,128)(2,1)S(1)}, bf16[96,1024]{1,0:T(8,128)(2,1)S(1)}, u32[]{:S(2)}, u32[]{:S(2)}) collective-permute-start(bf16[96,1024]{1,0:T(8,128)(2,1)S(1)} %constant_dynamic-update-slice_fusion.2.refs_1_), channel_id=1, source_target_pairs={{0,1},{1,0},{2,3},{3,2},{4,5},{5,4},{6,7},{7,6},{8,9},{9,8},{10,11... | collective-permute-start | bytes 589832 | tf_op jit(solution)/shard_map/ppermute | solution.py:327
